TPU v7x, 32 devices: a whole 2x2x4 slice. The times are simulated.
32 devices in a mesh: groups: 2 (over y), queue: 8 (over z, x), tp: 2 (over core).
Axes of the slice: x: 2, y: 2, z: 4, core: 2. Of those that a mesh axis runs over, the one named last changes fastest.
Arguments:
- hidden: bfloat16 [3328, 5120], P(('groups', 'queue'), 'tp'), parts along dimension 0, may hold values from -8 to 8
- q_weight: bfloat16 [1, 40, 128, 128], P(None, 'tp'), may hold values from -1 to 2.5
- k_weight: bfloat16 [1, 40, 128, 128], P(None, 'tp'), may hold values from -1 to 2.5
- v_weight: bfloat16 [1, 40, 128, 128], P(None, 'tp'), may hold values from -0.5 to 0.5
- mod_base: float32 [1, 3, 5120], P(None, None, 'tp'), may hold values from -3 to 3
- mod_amp: float32 [1, 3, 5120], P(None, None, 'tp'), may hold values from -3 to 3
- levels: int32 [16], P(('groups', 'queue')), parts along dimension 0, may hold values from 0 to 63
- steps_table: int32 [65], replicated, may hold values from 0 to 1000
- group_pos: int32 [16], P('groups'), parts along dimension 0, may hold values from 0 to 31
Outputs:
- new_queue: bfloat16 [3328, 5120], P(('groups', 'queue'), 'tp'), parts along dimension 0
- velocity: bfloat16 [3328, 5120], P(('groups', 'queue'), 'tp'), parts along dimension 0
There are 2 independent parts, one for each index of `groups`. A program takes and returns all parts, laid end to end along the dimension named above; an argument that names none is the same for every part. Nothing has to cross between parts.
All inputs are finite; a program needn't handle non-finite values.
Results may differ from a plain program's by a relative error of at most 0.0054.
Values may be sent and summed in bfloat16 or wider, within the bound.
A program may use at most 64 MiB of HBM per device.

v0:
```python
import functools
import math

import jax
import jax.numpy as jnp
from jax import lax
from jax.experimental import pallas as pl
from jax.experimental.pallas import tpu as pltpu
from jax.sharding import PartitionSpec as P

HEAD = 128
D = 5120
WIDE = 52
HW_DEV = 104
F32 = jnp.float32
BF16 = jnp.bfloat16


def time_embed(moment, channel):
    within = channel % 256
    freq = jnp.exp(-jnp.log(10000.0) * (within % 128).astype(F32) / 128.0)
    angle = moment * freq
    return jnp.where(within < 128, jnp.cos(angle), jnp.sin(angle))


def turn_tables(starts, count):
    place = jnp.arange(count, dtype=jnp.int32)
    inner = place % HW_DEV
    frame = (place // HW_DEV)[:, None]
    hpos = (inner // WIDE).astype(F32)[:, None]
    wpos = (inner % WIDE).astype(F32)[:, None]
    lane = jnp.arange(HEAD, dtype=jnp.int32)
    pair = lane // 2
    side = HEAD // 6
    time = (HEAD - 4 * side) // 2
    freq_t = 10000.0 ** (-pair.astype(F32) / time)
    freq_h = 10000.0 ** (-(pair - time).astype(F32) / side)
    freq_w = 10000.0 ** (-(pair - time - side).astype(F32) / side)
    tpos = (starts[:, None, None] + frame[None]).astype(F32)
    on_t = (pair < time)[None, None, :]
    on_h = (pair < time + side)[None, None, :]
    angle = jnp.where(
        on_t,
        tpos * freq_t[None, None, :],
        jnp.where(on_h, (hpos * freq_h[None, :])[None], (wpos * freq_w[None, :])[None]),
    )
    sign = jnp.where(lane % 2 == 0, -1.0, 1.0).astype(F32)
    return jnp.cos(angle), jnp.sin(angle) * sign[None, None, :]


def kernel(
    chunks, length,
    hid, wq, wk, wv, mods, sendmods, cost, sint,
    newq, vel,
    near, far, nmods, fmods, tsend, trecv, nstat, fstat, ostat,
    qrot, krot, vown, wk2, qsq, ksq, adv, kcat, vcat,
    hs, hr, fs, fr, tss, trs, mss, mrs, sss, srs, avs, avr,
):
    rows, width = hid.shape
    heads = width // HEAD
    per = heads // chunks
    cw = per * HEAD
    me = lax.axis_index("queue")
    core = lax.axis_index("tp")
    odd = lax.rem(me, 2)
    s = 1 - 2 * odd
    has_far = jnp.logical_and(me - s >= 0, me - s < length)
    has_fwd = jnp.logical_and(me + 2 * s >= 0, me + 2 * s < length)
    has_src = has_far

    def clip(j):
        return jnp.minimum(jnp.maximum(j, 0), length - 1)

    dev_near = {"queue": clip(me + s)}
    dev_far = {"queue": clip(me - s)}
    dev_fwd = {"queue": clip(me + 2 * s)}
    dev_src = {"queue": clip(me - 2 * s)}
    dev_next = {"queue": clip(me + 1)}
    partner = {"tp": 1 - core}
    MESH = pl.DeviceIdType.MESH

    barrier = pltpu.get_barrier_semaphore()
    pl.semaphore_signal(barrier, inc=1, device_id=partner, device_id_type=MESH)
    pl.semaphore_signal(barrier, inc=1, device_id=dev_near, device_id_type=MESH)

    @pl.when(has_far)
    def _():
        pl.semaphore_signal(barrier, inc=1, device_id=dev_far, device_id_type=MESH)
        pl.semaphore_signal(barrier, inc=1, device_id=dev_src, device_id_type=MESH)

    @pl.when(has_fwd)
    def _():
        pl.semaphore_signal(barrier, inc=1, device_id=dev_fwd, device_id_type=MESH)

    peers = 2 + jnp.where(has_far, 2, 0) + jnp.where(has_fwd, 1, 0)
    pl.semaphore_wait(barrier, peers)

    def cols(c):
        return pl.ds(pl.multiple_of(c * cw, cw), cw)

    def hcols(h):
        return pl.ds(pl.multiple_of(h * HEAD, HEAD), HEAD)

    def remote(src, dst, ss, rs, dev):
        return pltpu.make_async_remote_copy(
            src_ref=src, dst_ref=dst, send_sem=ss, recv_sem=rs, device_id=dev, device_id_type=MESH
        )

    def hid_copy(c):
        return remote(hid.at[:, cols(c)], near.at[:, cols(c)], hs.at[c], hr.at[c], dev_near)

    def fwd_copy(c):
        return remote(near.at[:, cols(c)], far.at[:, cols(c)], fs.at[c], fr.at[c], dev_fwd)

    def adv_copy(c):
        return remote(adv.at[:, cols(c)], newq.at[:, cols(c)], avs.at[c], avr.at[c], dev_next)

    mod_near = remote(sendmods, nmods, mss.at[0], mrs.at[0], dev_near)
    mod_far = remote(sendmods, fmods, mss.at[1], mrs.at[1], dev_far)
    stat_near = remote(ostat, nstat, sss.at[0], srs.at[0], dev_near)
    stat_far = remote(ostat, fstat, sss.at[1], srs.at[1], dev_far)
    tot0 = remote(tsend.at[0:2], trecv.at[0:2], tss.at[0], trs.at[0], partner)
    tot1 = remote(tsend.at[2:4], trecv.at[2:4], tss.at[1], trs.at[1], partner)

    mod_near.start()

    @pl.when(has_far)
    def _():
        mod_far.start()

    @pl.loop(0, chunks)
    def _(c):
        hid_copy(c).start()

    def forward(c):
        hid_copy(c).wait_recv()

        @pl.when(has_fwd)
        def _():
            fwd_copy(c).start()

    tsend[0] = jnp.zeros((rows, HEAD), F32)
    tsend[1] = jnp.zeros((rows, HEAD), F32)

    @pl.loop(0, heads)
    def _(h):
        x = hid[:, hcols(h)].astype(F32)
        tsend[0] += x
        tsend[1] += x * x

    tot0.start()

    lane = lax.broadcasted_iota(jnp.int32, (rows, HEAD), 1)
    swap = (
        lax.broadcasted_iota(jnp.int32, (HEAD, HEAD), 0)
        == (lax.broadcasted_iota(jnp.int32, (HEAD, HEAD), 1) ^ 1)
    ).astype(F32).astype(BF16)
    keys = kcat.shape[0]
    kcat[3 * rows:, :] = jnp.zeros((keys - 3 * rows, HEAD), BF16)
    vcat[:, HEAD:] = jnp.ones((keys, HEAD), BF16)
    vcat[3 * rows:, :HEAD] = jnp.zeros((keys - 3 * rows, HEAD), BF16)
    key_lane = lax.broadcasted_iota(jnp.int32, (1, keys), 1)
    limit = jnp.where(has_far, 3 * rows, 2 * rows)
    bias = jnp.where(key_lane < limit, 0.0, -1e30).astype(F32)

    @pl.when(jnp.logical_not(has_far))
    def _():
        far[...] = jnp.zeros_like(far)
        fmods[...] = jnp.zeros_like(fmods)
        fstat[...] = jnp.zeros_like(fstat)

    @pl.when(me == 0)
    def _():
        newq[...] = jnp.zeros_like(newq)

    qsq[...] = jnp.zeros_like(qsq)
    ksq[...] = jnp.zeros_like(ksq)
    tot0.wait()
    total = jnp.sum(tsend[0] + trecv[0], axis=1, keepdims=True)
    second = jnp.sum(tsend[1] + trecv[1], axis=1, keepdims=True)
    mean = total / D
    rstd = lax.rsqrt(second / D - mean * mean + 1e-06)
    ostat[...] = jnp.where(lane == 0, mean, rstd)

    def mix(x, mu, rs, scale, shift):
        return ((x.astype(F32) - mu) * rs * (1.0 + scale) + shift).astype(BF16)

    def dot(a, b):
        return jnp.dot(a, b, preferred_element_type=F32)

    def own(h):
        mu = ostat[:, 0:1]
        rs = ostat[:, 1:2]
        mixed = mix(hid[:, hcols(h)], mu, rs, mods[1:2, hcols(h)], mods[0:1, hcols(h)])
        q = wq[h]
        k = wk[h]
        q2 = jnp.concatenate([q, dot(q, swap).astype(BF16)], axis=1)
        k2 = jnp.concatenate([k, dot(k, swap).astype(BF16)], axis=1)
        wk2[h] = k2
        qraw = dot(mixed, q2)
        kraw = dot(mixed, k2)
        q1 = qraw[:, :HEAD]
        k1 = kraw[:, :HEAD]
        qsq[...] += q1 * q1
        ksq[...] += k1 * k1
        qrot[h] = q1 * cost[0] + qraw[:, HEAD:] * sint[0]
        krot[h] = k1 * cost[0] + kraw[:, HEAD:] * sint[0]
        vown[h] = dot(mixed, wv[h]).astype(BF16)

    half = heads // 2

    @pl.loop(0, half)
    def _(h):
        own(h)

    ahead = min(3, chunks)
    forward(0)

    @pl.loop(half, heads)
    def _(h):
        own(h)

    tsend[2] = qsq[...]
    tsend[3] = ksq[...]
    tot1.start()

    @pl.loop(1, ahead)
    def _(c):
        forward(c)

    tot1.wait()
    qt = jnp.sum(tsend[2] + trecv[2], axis=1, keepdims=True)
    kt = jnp.sum(tsend[3] + trecv[3], axis=1, keepdims=True)
    rq = lax.rsqrt(qt / D + 1e-06)
    rk = lax.rsqrt(kt / D + 1e-06)
    qsq[...] = jnp.broadcast_to(rq, (rows, HEAD))
    ksq[...] = jnp.broadcast_to(rk, (rows, HEAD))
    ostat[...] = jnp.where(lane == 2, rk, ostat[...])
    stat_near.start()

    @pl.when(has_far)
    def _():
        stat_far.start()

    mod_near.wait()
    stat_near.wait()

    @pl.when(has_far)
    def _():
        mod_far.wait()
        stat_far.wait()

    factor = math.log2(math.e) / math.sqrt(HEAD)

    def other(h, slot, buf, stat, md):
        mixed = mix(buf[:, hcols(h)], stat[:, 0:1], stat[:, 1:2], md[1:2, hcols(h)], md[0:1, hcols(h)])
        kraw = dot(mixed, wk2[h])
        rk = stat[:, 2:3]
        turned = kraw[:, :HEAD] * cost[slot] + kraw[:, HEAD:] * sint[slot]
        kcat[slot * rows:(slot + 1) * rows, :] = (turned * rk).astype(BF16)
        vcat[slot * rows:(slot + 1) * rows, :HEAD] = dot(mixed, wv[h]).astype(BF16)

    def head(h):
        query = (qrot[h] * qsq[...]).astype(BF16)
        kcat[0:rows, :] = (krot[h] * ksq[...]).astype(BF16)
        vcat[0:rows, :HEAD] = vown[h]
        other(h, 1, near, nstat, nmods)
        other(h, 2, far, fstat, fmods)
        scores = lax.dot_general(
            query, kcat[...], (((1,), (1,)), ((), ())), preferred_element_type=F32
        )
        scores = scores * factor + bias
        top = jnp.max(scores, axis=1, keepdims=True)
        weights = jnp.exp2(scores - top).astype(BF16)
        out = dot(weights, vcat[...])
        attn = out[:, :HEAD] / out[:, HEAD:]
        x = hid[:, hcols(h)].astype(F32)
        state = x + mods[2:3, hcols(h)] * attn
        vel[:, hcols(h)] = state.astype(BF16)
        adv[:, hcols(h)] = (x + mods[3:4, hcols(h)] * state).astype(BF16)

    has_next = me < length - 1

    @pl.loop(0, chunks)
    def _(c):
        @pl.when(c + ahead < chunks)
        def _():
            forward(c + ahead)

        @pl.when(has_far)
        def _():
            fwd_copy(c).wait_recv()

        @pl.loop(0, per)
        def _(n):
            head(c * per + n)

        @pl.when(jnp.logical_and(has_next, c > 0))
        def _():
            adv_copy(c - 1).start()

    @pl.when(has_next)
    def _():
        adv_copy(chunks - 1).start()

    @pl.loop(0, chunks)
    def _(c):
        hid_copy(c).wait_send()

        @pl.when(has_fwd)
        def _():
            fwd_copy(c).wait_send()

        @pl.when(has_next)
        def _():
            adv_copy(c).wait_send()

        @pl.when(me > 0)
        def _():
            adv_copy(c).wait_recv()


def body(length, hidden, q_weight, k_weight, v_weight, mod_base, mod_amp, levels, steps_table, group_pos):
    rows, width = hidden.shape
    heads = width // HEAD
    chunks = next(n for n in (10, 5, 4, 2, 1) if heads % n == 0)
    position = lax.axis_index("queue")
    t_now = steps_table[levels[0]].astype(F32)
    t_next = steps_table[levels[0] + 1].astype(F32)
    channel = lax.axis_index("tp") * width + jnp.arange(width, dtype=jnp.int32)
    emb = time_embed(t_now, channel)
    mods = mod_base[0] + mod_amp[0] * emb[None, :]
    step = jnp.full((1, width), (t_next - t_now) / 1000.0, F32)
    sendmods = mods[:2]
    mods = jnp.concatenate([mods, step], axis=0)
    s = 1 - 2 * (position % 2)
    slots = jnp.stack([position, position + s, position - s])
    starts = group_pos[jnp.clip(slots, 0, length - 1)]
    cost, sint = turn_tables(starts, rows)
    keys = -(-3 * rows // 128) * 128
    vmem = pl.BlockSpec(memory_space=pltpu.VMEM)
    dma = pltpu.SemaphoreType.DMA
    return pl.pallas_call(
        functools.partial(kernel, chunks, length),
        name="denoise",
        out_shape=(
            jax.ShapeDtypeStruct((rows, width), BF16),
            jax.ShapeDtypeStruct((rows, width), BF16),
        ),
        in_specs=[vmem] * 8,
        out_specs=(vmem, vmem),
        scratch_shapes=[
            pltpu.VMEM((rows, width), BF16),
            pltpu.VMEM((rows, width), BF16),
            pltpu.VMEM((2, width), F32),
            pltpu.VMEM((2, width), F32),
            pltpu.VMEM((4, rows, HEAD), F32),
            pltpu.VMEM((4, rows, HEAD), F32),
            pltpu.VMEM((rows, HEAD), F32),
            pltpu.VMEM((rows, HEAD), F32),
            pltpu.VMEM((rows, HEAD), F32),
            pltpu.VMEM((heads, rows, HEAD), F32),
            pltpu.VMEM((heads, rows, HEAD), F32),
            pltpu.VMEM((heads, rows, HEAD), BF16),
            pltpu.VMEM((heads, HEAD, 2 * HEAD), BF16),
            pltpu.VMEM((rows, HEAD), F32),
            pltpu.VMEM((rows, HEAD), F32),
            pltpu.VMEM((rows, width), BF16),
            pltpu.VMEM((keys, HEAD), BF16),
            pltpu.VMEM((keys, 2 * HEAD), BF16),
            dma((chunks,)), dma((chunks,)), dma((chunks,)), dma((chunks,)),
            dma((2,)), dma((2,)), dma((2,)), dma((2,)), dma((2,)), dma((2,)),
            dma((chunks,)), dma((chunks,)),
        ],
        compiler_params=pltpu.CompilerParams(
            collective_id=0, has_side_effects=True, vmem_limit_bytes=48 * 1024 * 1024
        ),
    )(hidden, q_weight[0], k_weight[0], v_weight[0], mods, sendmods, cost, sint)


def solution(mesh):
    length = mesh.shape["queue"]
    return jax.shard_map(
        functools.partial(body, length),
        mesh=mesh,
        in_specs=(
            P(("groups", "queue"), "tp"),
            P(None, "tp", None, None),
            P(None, "tp", None, None),
            P(None, "tp", None, None),
            P(None, None, "tp"),
            P(None, None, "tp"),
            P(("groups", "queue")),
            P(),
            P("groups"),
        ),
        out_specs=(P(("groups", "queue"), "tp"), P(("groups", "queue"), "tp")),
        check_vma=False,
    )
```

profile of v0, /device:TPU:18, one launch (start us, length us, event | category | flops | bytes accessed | tf_op | source)
XLA Modules:
  0.0 71.2 jit_solution(8710325380396792006)
XLA Ops:
  0.6 0.0 copy-start
  0.6 0.0 copy-start.2
  0.7 0.0 copy-start.1
  1.5 0.1 fusion.15
  1.5 1.3 %fusion.16 = (s32[1]{0:T(128)}, s32[1]{0:T(128)}) fusion(s32[65]{0:T(128)} %param.16, s32[]{:T(128)S(6)} %select_n.147, s32[]{:T(128)S(6)} %select_n.144), kind=kLoop, calls=%fused_computation.51 | loop fusion | bytes 24 | tf_op jit(solution)/shard_map/dynamic_slice | solution.py:329
  4.3 0.0 copy-done
  4.3 0.6 gather_fusion
  4.9 0.1 add_convert_fusion
  5.0 0.1 sine_select_fusion
  5.1 0.8 %fusion.1 = f32[3,2560]{1,0:T(4,128)S(1)} fusion(f32[1,3,2560]{2,0,1:T(1,128)} %param.14, f32[1,3,2560]{2,0,1:T(1,128)} %param.13, f32[2560]{0:T(1024)S(1)} %sine_select_fusion), kind=kLoop, calls=%fused_computation.6 | loop fusion | flops 15360 | bytes 102400 | tf_op jit(solution)/shard_map/add | solution.py:332
  5.9 0.1 multiply_select_fusion.1
  6.0 1.2 %sine_multiply_fusion = (f32[3,208,128]{2,1,0:T(8,128)S(1)}, f32[3,208,128]{2,1,0:T(8,128)S(1)}) fusion(f32[128]{0:T(128)S(1)} %get-tuple-element.10, f32[208,128]{1,0:T(8,128)S(1)} %multiply_select_fusion.1, f32[128]{0:T(128)S(1)} %get-tuple-element.11, f32[3,208]{1,0:T(4,128)S(1)} %add_convert_fusion, pred[128]{0:T(512)(128)(4,1)S(1)} %broadcast_compare_fusion.1), kind=kLoop, calls=%fused_computation.1 | loop fusion | flops 239616 | bytes 749120 | tf_op jit(solution)/shard_map/mul | solution.py:48
  7.2 0.0 copy-done.2
  7.3 0.0 copy-done.1
  7.3 0.0 copy-start.3
  7.3 1.1 %copy-done.3 = bf16[1,20,128,128]{3,2,1,0:T(8,128)(2,1)S(1)} copy-done((bf16[1,20,128,128]{3,2,1,0:T(8,128)(2,1)S(1)}, bf16[1,20,128,128]{3,2,1,0:T(8,128)(2,1)}, u32[]{:S(2)}) %copy-start.3) | copy-done | bytes 655384
  8.4 0.0 copy-start.4
  8.4 1.1 %copy-done.4 = bf16[1,20,128,128]{3,2,1,0:T(8,128)(2,1)S(1)} copy-done((bf16[1,20,128,128]{3,2,1,0:T(8,128)(2,1)S(1)}, bf16[1,20,128,128]{3,2,1,0:T(8,128)(2,1)}, u32[]{:S(2)}) %copy-start.4) | copy-done | bytes 655384
  9.4 59.8 %denoise.1 = (bf16[208,2560]{1,0:T(8,128)(2,1)S(1)}, bf16[208,2560]{1,0:T(8,128)(2,1)S(1)}) custom-call(bf16[208,2560]{1,0:T(8,128)(2,1)S(1)} %copy-done.1, bf16[20,128,128]{2,1,0:T(8,128)(2,1)S(1)} %bitcast.22, bf16[20,128,128]{2,1,0:T(8,128)(2,1)S(1)} %bitcast.23, bf16[20,128,128]{2,1,0:T(8,128)(2,1)S(1)} %bitcast.24, f32[4,2560]{1,0:T(4,128)S(1)} %concatenate.10.mods, ...), custom_call_target="tpu_custom_call" | custom-call | tf_op jit(solution)/shard_map/denoise/pallas_call | solution.py:343
  69.3 1.0 %copy.18 = bf16[208,2560]{1,0:T(8,128)(2,1)} copy(bf16[208,2560]{1,0:T(8,128)(2,1)S(1)} %get-tuple-element.14) | data formatting | bytes 2129920
  70.3 1.0 %copy.19 = bf16[208,2560]{1,0:T(8,128)(2,1)} copy(bf16[208,2560]{1,0:T(8,128)(2,1)S(1)} %get-tuple-element.15) | data formatting | bytes 2129920
  (9 shorter events, 0.1 us)
Async XLA Ops:
  0.6 3.6 %copy-start = (s32[8]{0:T(128)S(1)}, s32[8]{0:T(128)}, u32[]{:S(2)}) copy-start(s32[8]{0:T(128)} %param.17) | copy-start | bytes 100
  0.6 6.6 %copy-start.2 = (bf16[1,20,128,128]{3,2,1,0:T(8,128)(2,1)S(1)}, bf16[1,20,128,128]{3,2,1,0:T(8,128)(2,1)}, u32[]{:S(2)}) copy-start(bf16[1,20,128,128]{3,2,1,0:T(8,128)(2,1)} %param.10) | copy-start | bytes 1966084
  0.7 6.6 %copy-start.1 = (bf16[208,2560]{1,0:T(8,128)(2,1)S(1)}, bf16[208,2560]{1,0:T(8,128)(2,1)}, u32[]{:S(2)}) copy-start(bf16[208,2560]{1,0:T(8,128)(2,1)} %hid.1) | copy-start | bytes 3194884
  7.3 1.1 %copy-start.3 = (bf16[1,20,128,128]{3,2,1,0:T(8,128)(2,1)S(1)}, bf16[1,20,128,128]{3,2,1,0:T(8,128)(2,1)}, u32[]{:S(2)}) copy-start(bf16[1,20,128,128]{3,2,1,0:T(8,128)(2,1)} %param.11) | copy-start | bytes 1966084
  8.4 1.1 %copy-start.4 = (bf16[1,20,128,128]{3,2,1,0:T(8,128)(2,1)S(1)}, bf16[1,20,128,128]{3,2,1,0:T(8,128)(2,1)}, u32[]{:S(2)}) copy-start(bf16[1,20,128,128]{3,2,1,0:T(8,128)(2,1)} %param.12) | copy-start | bytes 1966084
where the time goes:
time: 71.6 us; the launch traced here: 71.2 us
  Pallas kernels  59.8 us (84%)
  local copies, waits for them, and re-layouts  6.12 us (9%)
  between operations  2.87 us (4%)
  other arithmetic  2.42 us (3%)
    pallas_call x1, Pallas kernels, body(): pl.pallas_call(functools.partial(kernel, chunks, length), name='denoise',...  59.8 us
    unnamed x12, local copies, waits for them, and re-layouts  4.14 us

commit v1 on v0

--- a/solution.py
+++ b/solution.py
@@ -16,50 +16,35 @@
 BF16 = jnp.bfloat16
 
 
-def time_embed(moment, channel):
-    within = channel % 256
-    freq = jnp.exp(-jnp.log(10000.0) * (within % 128).astype(F32) / 128.0)
-    angle = moment * freq
-    return jnp.where(within < 128, jnp.cos(angle), jnp.sin(angle))
-
-
-def turn_tables(starts, count):
-    place = jnp.arange(count, dtype=jnp.int32)
-    inner = place % HW_DEV
-    frame = (place // HW_DEV)[:, None]
-    hpos = (inner // WIDE).astype(F32)[:, None]
-    wpos = (inner % WIDE).astype(F32)[:, None]
-    lane = jnp.arange(HEAD, dtype=jnp.int32)
-    pair = lane // 2
+def turn_freq():
+    pair = jnp.arange(HEAD, dtype=jnp.int32) // 2
     side = HEAD // 6
     time = (HEAD - 4 * side) // 2
     freq_t = 10000.0 ** (-pair.astype(F32) / time)
     freq_h = 10000.0 ** (-(pair - time).astype(F32) / side)
     freq_w = 10000.0 ** (-(pair - time - side).astype(F32) / side)
-    tpos = (starts[:, None, None] + frame[None]).astype(F32)
-    on_t = (pair < time)[None, None, :]
-    on_h = (pair < time + side)[None, None, :]
-    angle = jnp.where(
-        on_t,
-        tpos * freq_t[None, None, :],
-        jnp.where(on_h, (hpos * freq_h[None, :])[None], (wpos * freq_w[None, :])[None]),
-    )
-    sign = jnp.where(lane % 2 == 0, -1.0, 1.0).astype(F32)
-    return jnp.cos(angle), jnp.sin(angle) * sign[None, None, :]
+    return jnp.where(pair < time, freq_t, jnp.where(pair < time + side, freq_h, freq_w))[None]
 
 
 def kernel(
     chunks, length,
-    hid, wq, wk, wv, mods, sendmods, cost, sint,
+    hid_in, wq_in, wk_in, wv_in, base, amp, cfreq, tfreq, levels, steps, gpos,
     newq, vel,
     near, far, nmods, fmods, tsend, trecv, nstat, fstat, ostat,
     qrot, krot, vown, wk2, qsq, ksq, adv, kcat, vcat,
+    hid, wq, wk, wv, mods, sendmods, cost, sint, mstat, wide, ins,
     hs, hr, fs, fr, tss, trs, mss, mrs, sss, srs, avs, avr,
 ):
-    rows, width = hid.shape
+    rows, width = hid_in.shape
     heads = width // HEAD
     per = heads // chunks
     cw = per * HEAD
+    loads = [
+        pltpu.make_async_copy(src, dst, ins.at[n])
+        for n, (src, dst) in enumerate(((hid_in, hid), (wq_in, wq), (wk_in, wk), (wv_in, wv)))
+    ]
+    for load in loads:
+        load.start()
     me = lax.axis_index("queue")
     core = lax.axis_index("tp")
     odd = lax.rem(me, 2)
@@ -117,20 +102,26 @@
 
     mod_near = remote(sendmods, nmods, mss.at[0], mrs.at[0], dev_near)
     mod_far = remote(sendmods, fmods, mss.at[1], mrs.at[1], dev_far)
-    stat_near = remote(ostat, nstat, sss.at[0], srs.at[0], dev_near)
-    stat_far = remote(ostat, fstat, sss.at[1], srs.at[1], dev_far)
+    stat_near = remote(mstat, nstat, sss.at[0], srs.at[0], dev_near)
+    stat_far = remote(mstat, fstat, sss.at[1], srs.at[1], dev_far)
     tot0 = remote(tsend.at[0:2], trecv.at[0:2], tss.at[0], trs.at[0], partner)
     tot1 = remote(tsend.at[2:4], trecv.at[2:4], tss.at[1], trs.at[1], partner)
 
-    mod_near.start()
-
-    @pl.when(has_far)
-    def _():
-        mod_far.start()
+    loads[0].wait()
 
     @pl.loop(0, chunks)
     def _(c):
         hid_copy(c).start()
+
+    now = steps[levels[0]].astype(F32)
+    ahead_t = steps[levels[0] + 1].astype(F32)
+    channel = lax.broadcasted_iota(jnp.int32, (1, width), 1) + core * width
+    phase = cfreq[...] * now
+    emb = jnp.where((channel & 255) < 128, jnp.cos(phase), jnp.sin(phase))
+    own_mods = base[...] + amp[...] * emb
+    sendmods[...] = own_mods[0:2]
+    mods[0:3] = own_mods
+    mods[3:4] = jnp.broadcast_to((ahead_t - now) / 1000.0, (1, width))
 
     def forward(c):
         hid_copy(c).wait_recv()
@@ -149,6 +140,32 @@
         tsend[1] += x * x
 
     tot0.start()
+    mod_near.start()
+
+    @pl.when(has_far)
+    def _():
+        mod_far.start()
+
+    place = lax.broadcasted_iota(jnp.int32, (rows, HEAD), 0)
+    frame = jnp.zeros_like(place)
+    for n in range(1, rows // HW_DEV):
+        frame += (place >= n * HW_DEV).astype(jnp.int32)
+    inner = place - frame * HW_DEV
+    hpos = jnp.zeros_like(place)
+    for n in range(1, HW_DEV // WIDE):
+        hpos += (inner >= n * WIDE).astype(jnp.int32)
+    wpos = inner - hpos * WIDE
+    spot = lax.broadcasted_iota(jnp.int32, (rows, HEAD), 1)
+    pair = lax.shift_right_logical(spot, 1)
+    side = HEAD // 6
+    time = (HEAD - 4 * side) // 2
+    rest = jnp.where(pair < time + side, hpos, wpos)
+    sign = jnp.where((spot & 1) == 0, -1.0, 1.0).astype(F32)
+    for slot, owner in enumerate((me, me + s, me - s)):
+        moment = jnp.where(pair < time, gpos[clip(owner)] + frame, rest).astype(F32)
+        angle = moment * tfreq[...]
+        cost[slot] = jnp.cos(angle)
+        sint[slot] = jnp.sin(angle) * sign
 
     lane = lax.broadcasted_iota(jnp.int32, (rows, HEAD), 1)
     swap = (
@@ -207,6 +224,9 @@
         krot[h] = k1 * cost[0] + kraw[:, HEAD:] * sint[0]
         vown[h] = dot(mixed, wv[h]).astype(BF16)
 
+    for load in loads[1:]:
+        load.wait()
+
     half = heads // 2
 
     @pl.loop(0, half)
@@ -236,6 +256,9 @@
     qsq[...] = jnp.broadcast_to(rq, (rows, HEAD))
     ksq[...] = jnp.broadcast_to(rk, (rows, HEAD))
     ostat[...] = jnp.where(lane == 2, rk, ostat[...])
+    wide[...] = jnp.zeros_like(wide)
+    wide[0:rows] = ostat[...]
+    mstat[...] = jnp.transpose(wide[...])[0:8]
     stat_near.start()
 
     @pl.when(has_far)
@@ -249,6 +272,15 @@
     def _():
         mod_far.wait()
         stat_far.wait()
+
+    def spread(stat, place_at):
+        full = jnp.concatenate([stat[...], jnp.zeros((HEAD - 8, stat.shape[1]), F32)], axis=0)
+        place_at[...] = jnp.transpose(full)[0:rows]
+
+    spread(nstat, trecv.at[0])
+    spread(fstat, trecv.at[1])
+    near_stat = trecv.at[0]
+    far_stat = trecv.at[1]
 
     factor = math.log2(math.e) / math.sqrt(HEAD)
 
@@ -264,8 +296,8 @@
         query = (qrot[h] * qsq[...]).astype(BF16)
         kcat[0:rows, :] = (krot[h] * ksq[...]).astype(BF16)
         vcat[0:rows, :HEAD] = vown[h]
-        other(h, 1, near, nstat, nmods)
-        other(h, 2, far, fstat, fmods)
+        other(h, 1, near, near_stat, nmods)
+        other(h, 2, far, far_stat, fmods)
         scores = lax.dot_general(
             query, kcat[...], (((1,), (1,)), ((), ())), preferred_element_type=F32
         )
@@ -324,19 +356,10 @@
     rows, width = hidden.shape
     heads = width // HEAD
     chunks = next(n for n in (10, 5, 4, 2, 1) if heads % n == 0)
-    position = lax.axis_index("queue")
-    t_now = steps_table[levels[0]].astype(F32)
-    t_next = steps_table[levels[0] + 1].astype(F32)
     channel = lax.axis_index("tp") * width + jnp.arange(width, dtype=jnp.int32)
-    emb = time_embed(t_now, channel)
-    mods = mod_base[0] + mod_amp[0] * emb[None, :]
-    step = jnp.full((1, width), (t_next - t_now) / 1000.0, F32)
-    sendmods = mods[:2]
-    mods = jnp.concatenate([mods, step], axis=0)
-    s = 1 - 2 * (position % 2)
-    slots = jnp.stack([position, position + s, position - s])
-    starts = group_pos[jnp.clip(slots, 0, length - 1)]
-    cost, sint = turn_tables(starts, rows)
+    within = channel % 256
+    cfreq = jnp.exp(-jnp.log(10000.0) * (within % 128).astype(F32) / 128.0)[None]
+    tall = -(-rows // 128) * 128
     keys = -(-3 * rows // 128) * 128
     vmem = pl.BlockSpec(memory_space=pltpu.VMEM)
     dma = pltpu.SemaphoreType.DMA
@@ -347,7 +370,9 @@
             jax.ShapeDtypeStruct((rows, width), BF16),
             jax.ShapeDtypeStruct((rows, width), BF16),
         ),
-        in_specs=[vmem] * 8,
+        in_specs=[pl.BlockSpec(memory_space=pl.ANY)] * 4
+        + [vmem] * 4
+        + [pl.BlockSpec(memory_space=pltpu.SMEM)] * 3,
         out_specs=(vmem, vmem),
         scratch_shapes=[
             pltpu.VMEM((rows, width), BF16),
@@ -356,8 +381,8 @@
             pltpu.VMEM((2, width), F32),
             pltpu.VMEM((4, rows, HEAD), F32),
             pltpu.VMEM((4, rows, HEAD), F32),
-            pltpu.VMEM((rows, HEAD), F32),
-            pltpu.VMEM((rows, HEAD), F32),
+            pltpu.VMEM((8, tall), F32),
+            pltpu.VMEM((8, tall), F32),
             pltpu.VMEM((rows, HEAD), F32),
             pltpu.VMEM((heads, rows, HEAD), F32),
             pltpu.VMEM((heads, rows, HEAD), F32),
@@ -368,6 +393,17 @@
             pltpu.VMEM((rows, width), BF16),
             pltpu.VMEM((keys, HEAD), BF16),
             pltpu.VMEM((keys, 2 * HEAD), BF16),
+            pltpu.VMEM((rows, width), BF16),
+            pltpu.VMEM((heads, HEAD, HEAD), BF16),
+            pltpu.VMEM((heads, HEAD, HEAD), BF16),
+            pltpu.VMEM((heads, HEAD, HEAD), BF16),
+            pltpu.VMEM((4, width), F32),
+            pltpu.VMEM((2, width), F32),
+            pltpu.VMEM((3, rows, HEAD), F32),
+            pltpu.VMEM((3, rows, HEAD), F32),
+            pltpu.VMEM((8, tall), F32),
+            pltpu.VMEM((tall, HEAD), F32),
+            dma((4,)),
             dma((chunks,)), dma((chunks,)), dma((chunks,)), dma((chunks,)),
             dma((2,)), dma((2,)), dma((2,)), dma((2,)), dma((2,)), dma((2,)),
             dma((chunks,)), dma((chunks,)),
@@ -375,7 +411,10 @@
         compiler_params=pltpu.CompilerParams(
             collective_id=0, has_side_effects=True, vmem_limit_bytes=48 * 1024 * 1024
         ),
-    )(hidden, q_weight[0], k_weight[0], v_weight[0], mods, sendmods, cost, sint)
+    )(
+        hidden, q_weight[0], k_weight[0], v_weight[0], mod_base[0], mod_amp[0],
+        cfreq, turn_freq(), levels, steps_table, group_pos,
+    )
 
 
 def solution(mesh):

time: 71.6 us -> 67.5 us (0.943)
  Pallas kernels: 59.8 us -> 57.2 us
  local copies, waits for them, and re-layouts: 6.12 us -> 8.54 us
  other arithmetic: 2.42 us -> 0.11 us
  between operations: 2.87 us -> 1.32 us
    unnamed x12 -> x15, local copies, waits for them, and re-layouts: 4.14 us -> 8.54 us
    pallas_call x1, Pallas kernels: 59.8 us -> 57.2 us  [body(): pl.pallas_call(functools.partial(kernel, chunks, length), name='denoise',...]
    dynamic_slice x1 -> x0, local copies, waits for them, and re-layouts: 1.32 us -> none  [body(): t_next = steps_table[levels[0] + 1].astype(F32)]
    mul x1 -> x0, other arithmetic: 1.2 us -> none  [turn_tables(): return (jnp.cos(angle), jnp.sin(angle) * sign[None, None, :])]
    add x1 -> x0, other arithmetic: 0.8 us -> none  [body(): mods = mod_base[0] + mod_amp[0] * emb[None, :]]
where the time goes in v1:
time: 67.5 us; the launch traced here: 67.1 us
  Pallas kernels  57.2 us (85%)
  local copies, waits for them, and re-layouts  8.54 us (13%)
  between operations  1.32 us (2%)
    pallas_call x1, Pallas kernels, body(): pl.pallas_call(functools.partial(kernel, chunks, length), name='denoise',...  57.2 us
    unnamed x15, local copies, waits for them, and re-layouts  8.54 us

profile of v1, /device:TPU:18, one launch (start us, length us, event | category | flops | bytes accessed | tf_op | source)
XLA Modules:
  0.0 67.1 jit_solution(8081733939512812683)
XLA Ops:
  1.3 0.1 fusion.2.cfreq
  1.4 0.8 %copy_bitcast_fusion = (f32[3,2560]{1,0:T(4,128)S(1)}, f32[3,2560]{1,0:T(4,128)S(1)}) fusion(f32[1,3,2560]{2,0,1:T(1,128)} %param.14, f32[1,3,2560]{2,0,1:T(1,128)} %param.13), kind=kLoop, calls=%fused_computation.4 | loop fusion | bytes 122880
  2.2 0.0 copy-start
  2.2 1.2 %copy-done = bf16[208,2560]{1,0:T(8,128)(2,1)S(1)} copy-done((bf16[208,2560]{1,0:T(8,128)(2,1)S(1)}, bf16[208,2560]{1,0:T(8,128)(2,1)}, u32[]{:S(2)}) %copy-start) | copy-done | bytes 1064984
  3.4 0.0 copy-start.1
  3.4 1.1 %copy-done.1 = bf16[1,20,128,128]{3,2,1,0:T(8,128)(2,1)S(1)} copy-done((bf16[1,20,128,128]{3,2,1,0:T(8,128)(2,1)S(1)}, bf16[1,20,128,128]{3,2,1,0:T(8,128)(2,1)}, u32[]{:S(2)}) %copy-start.1) | copy-done | bytes 655384
  4.5 0.0 copy-start.2
  4.5 1.1 %copy-done.2 = bf16[1,20,128,128]{3,2,1,0:T(8,128)(2,1)S(1)} copy-done((bf16[1,20,128,128]{3,2,1,0:T(8,128)(2,1)S(1)}, bf16[1,20,128,128]{3,2,1,0:T(8,128)(2,1)}, u32[]{:S(2)}) %copy-start.2) | copy-done | bytes 655384
  5.6 0.0 copy-start.3
  5.6 1.1 %copy-done.3 = bf16[1,20,128,128]{3,2,1,0:T(8,128)(2,1)S(1)} copy-done((bf16[1,20,128,128]{3,2,1,0:T(8,128)(2,1)S(1)}, bf16[1,20,128,128]{3,2,1,0:T(8,128)(2,1)}, u32[]{:S(2)}) %copy-start.3) | copy-done | bytes 655384
  6.7 0.0 copy-start.4
  6.7 0.7 copy-done.4
  7.3 0.0 copy-start.5
  7.4 0.7 copy-done.5
  8.0 57.2 %denoise.1 = (bf16[208,2560]{1,0:T(8,128)(2,1)S(1)}, bf16[208,2560]{1,0:T(8,128)(2,1)S(1)}) custom-call(bf16[208,2560]{1,0:T(8,128)(2,1)S(1)} %copy-done, bf16[20,128,128]{2,1,0:T(8,128)(2,1)S(1)} %bitcast.7, bf16[20,128,128]{2,1,0:T(8,128)(2,1)S(1)} %bitcast.8, bf16[20,128,128]{2,1,0:T(8,128)(2,1)S(1)} %bitcast.9, f32[3,2560]{1,0:T(4,128)S(1)} %get-tuple-element.3.base, ...), custom_call_target="tpu_custom_call" | custom-call | tf_op jit(solution)/shard_map/denoise/pallas_call | solution.py:366
  65.2 1.0 %copy.18 = bf16[208,2560]{1,0:T(8,128)(2,1)} copy(bf16[208,2560]{1,0:T(8,128)(2,1)S(1)} %get-tuple-element.6) | data formatting | bytes 2129920
  66.2 1.0 %copy.19 = bf16[208,2560]{1,0:T(8,128)(2,1)} copy(bf16[208,2560]{1,0:T(8,128)(2,1)S(1)} %get-tuple-element.7) | data formatting | bytes 2129920
  (1 shorter events, 0.0 us)
Async XLA Ops:
  2.2 1.2 %copy-start = (bf16[208,2560]{1,0:T(8,128)(2,1)S(1)}, bf16[208,2560]{1,0:T(8,128)(2,1)}, u32[]{:S(2)}) copy-start(bf16[208,2560]{1,0:T(8,128)(2,1)} %hid_in.1) | copy-start | bytes 3194884
  3.4 1.1 %copy-start.1 = (bf16[1,20,128,128]{3,2,1,0:T(8,128)(2,1)S(1)}, bf16[1,20,128,128]{3,2,1,0:T(8,128)(2,1)}, u32[]{:S(2)}) copy-start(bf16[1,20,128,128]{3,2,1,0:T(8,128)(2,1)} %param.10) | copy-start | bytes 1966084
  4.5 1.1 %copy-start.2 = (bf16[1,20,128,128]{3,2,1,0:T(8,128)(2,1)S(1)}, bf16[1,20,128,128]{3,2,1,0:T(8,128)(2,1)}, u32[]{:S(2)}) copy-start(bf16[1,20,128,128]{3,2,1,0:T(8,128)(2,1)} %param.11) | copy-start | bytes 1966084
  5.6 1.1 %copy-start.3 = (bf16[1,20,128,128]{3,2,1,0:T(8,128)(2,1)S(1)}, bf16[1,20,128,128]{3,2,1,0:T(8,128)(2,1)}, u32[]{:S(2)}) copy-start(bf16[1,20,128,128]{3,2,1,0:T(8,128)(2,1)} %param.12) | copy-start | bytes 1966084
  6.7 0.7 copy-start.4
  7.3 0.7 copy-start.5
